TPU v7x, 32 devices: a whole 2x2x4 slice. The times are simulated.
32 devices in a mesh: row: 4 (over z), col: 8 (over y, x, core).
Axes of the slice: x: 2, y: 2, z: 4, core: 2. Of those that a mesh axis runs over, the one named last changes fastest.
Arguments:
- right_side: float32 [16, 1024, 3072], P(None, 'row', 'col'), may hold values from -100 to 100
- cond_x: float32 [1024, 3072], P('row', 'col'), may hold values from 0.25 to 4
- cond_y: float32 [1024, 3072], P('row', 'col'), may hold values from 0.25 to 4
- pad_mask: int32 [1024, 3072], P('row', 'col'), may hold values 0 or 1
Outputs:
- solution: float32 [16, 1024, 3072], P(None, 'row', 'col')
- residual: float32 [16, 1024, 3072], P(None, 'row', 'col')
All inputs are finite; a program needn't handle non-finite values. No bound on the sum of `pad_mask` on one device may be relied on, other than what follows from the above.
Results may differ from a plain program's by a relative error of at most 0.0003.
Values sent between devices are 32-bit elements; how exact they have to be, the bound alone decides.
A program may use at most 128 MiB of HBM per device.

v0:
```python
import jax
import jax.numpy as jnp
from jax import lax
from jax.sharding import PartitionSpec as P

ITERS = 3
exact_precision = lax.Precision.HIGHEST


def passed_along(shard, axis, by):
    peers = lax.axis_size(axis)
    pairs = [(i, i + by) for i in range(peers) if 0 <= i + by < peers]
    return lax.ppermute(shard, axis, pairs)


def extended(cells, sides, width):
    for axis, dim in sides:
        count = lax.axis_size(axis)
        ends = count - 1
        head = lax.slice_in_dim(cells, 0, width, axis=dim)
        tail = lax.slice_in_dim(cells, cells.shape[dim] - width, cells.shape[dim], axis=dim)
        cells = jnp.concatenate(
            [
                lax.ppermute(tail, axis, [(i, (i + 1) % count) for i in range(ends)]),
                cells,
                lax.ppermute(head, axis, [((i + 1) % count, i) for i in range(ends)]),
            ],
            axis=dim,
        )
    return cells


def neighbour_sum(padded, cond_x, cond_above, cond_y, cond_left):
    total = cond_x * padded[:, 2:, 1:-1] + cond_above * padded[:, :-2, 1:-1]
    return total + cond_y * padded[:, 1:-1, 2:] + cond_left * padded[:, 1:-1, :-2]


def gram(left, right):
    return jnp.einsum("kab,lab->kl", left, right, precision=exact_precision)


def combine(field, matrix):
    return jnp.einsum("kab,kl->lab", field, matrix, precision=exact_precision)


def small_solve(matrix, right):
    factor = jnp.linalg.cholesky(matrix)
    return jax.scipy.linalg.cho_solve((factor, True), right)


def shards(right_side, cond_x, cond_y, pad_mask):
    pad_nodes = pad_mask.astype(jnp.float32)
    free_nodes = 1.0 - pad_nodes
    upper_row = passed_along(cond_x[-1:], "row", 1)
    cond_above = jnp.concatenate([upper_row, cond_x[:-1]], 0)
    left_column = passed_along(cond_y[:, -1:], "col", 1)
    cond_left = jnp.concatenate([left_column, cond_y[:, :-1]], 1)
    diagonal = free_nodes * (cond_x + cond_above + cond_y + cond_left) + pad_nodes
    inverse = 1.0 / diagonal
    solution = jnp.zeros_like(right_side)
    residual = right_side
    precond = residual * inverse
    direction = precond
    gram_now = lax.psum(gram(residual, precond), ("row", "col"))
    for iteration in range(ITERS):
        padded = extended(free_nodes * direction, (("row", 1), ("col", 2)), 1)
        image = pad_nodes * direction + free_nodes * (
            diagonal * direction - neighbour_sum(padded, cond_x, cond_above, cond_y, cond_left)
        )
        weighted = image * inverse
        curvature, cross_term, image_term = lax.psum(
            (gram(direction, image), gram(image, precond), gram(image, weighted)), ("row", "col")
        )
        alpha_block = small_solve(curvature, gram_now)
        solution = solution + combine(direction, alpha_block)
        residual = residual - combine(image, alpha_block)
        precond = residual * inverse
        mixed = jnp.dot(alpha_block.T, cross_term, precision=exact_precision)
        quadratic = jnp.dot(
            jnp.dot(alpha_block.T, image_term, precision=exact_precision),
            alpha_block,
            precision=exact_precision,
        )
        gram_next = gram_now - mixed - mixed.T + quadratic
        beta_block = small_solve(gram_now, gram_next)
        direction = precond + combine(direction, beta_block)
        gram_now = gram_next
    return (solution, residual)


def solution(mesh):
    in_specs = (P(None, "row", "col"), P("row", "col"), P("row", "col"), P("row", "col"))
    out_specs = (P(None, "row", "col"), P(None, "row", "col"))
    return jax.shard_map(shards, mesh=mesh, in_specs=in_specs, out_specs=out_specs, check_vma=False)
```

profile of v0, /device:TPU:0, one launch (start us, length us, event | category | flops | bytes accessed | tf_op | source)
XLA Modules:
  0.0 509.1 jit_solution(3456726133904261827)
XLA Ops:
  1.3 4.9 collective-permute-start
  13.6 6.9 %multiply_multiply_fusion = f32[16,256,384]{2,0,1:T(8,128)S(1)} fusion(f32[16,256,384]{2,1,0:T(8,128)} %param.7, f32[256,384]{1,0:T(8,128)S(1)} %get-tuple-element.31, f32[256,384]{1,0:T(8,128)S(1)} %fusion.83), kind=kLoop, calls=%fused_computation.14 | loop fusion | flops 3145728 | bytes 13369344 | tf_op jit(solution)/shard_map/mul | solution.py:66
  20.5 3.5 collective-permute-start.3
  26.1 3.6 collective-permute-done.2
  37.6 3.6 collective-permute-start.5
  42.9 30.7 %fusion.78 = f32[16,16]{0,1:T(8,128)S(1)} fusion(f32[16,256,384]{2,1,0:T(8,128)} %param.7, f32[256,384]{1,0:T(8,128)S(1)} %fusion.83), kind=kOutput, calls=%fused_computation.115 | convolution fusion | flops 303562752 | bytes 6685696 | tf_op jit(solution)/shard_map/kab,lab->kl/dot_general | solution.py:39
  78.7 21.2 %fusion.14 = f32[16,256,384]{2,0,1:T(8,128)S(1)} fusion(f32[16,258,1]{2,0,1:T(8,128)} %copy.33, f32[16,1,384]{2,0,1:T(8,128)S(1)} %collective-permute-done.2, f32[16,256,384]{2,0,1:T(8,128)} %copy-done.2, f32[16,1,384]{2,0,1:T(8,128)S(1)} %collective-permute-done.3, f32[16,258,1]{2,0,1:T(8,128)} %copy.31, f32[16,256,384]{2,1,0:T(8,128)} %param.7, ...), kind=kLoop, calls=%fused_computation.17 | loop fusion | flops 33030144 | bytes 22102272 | tf_op jit(solution)/shard_map/add | solution.py:67
  99.9 8.1 %fusion.72 = f32[16,16]{1,0:T(8,128)S(1)} fusion(f32[16,256,384]{2,0,1:T(8,128)S(1)} %fusion.14, f32[256,384]{1,0:T(8,128)S(1)} %fusion.83), kind=kOutput, calls=%fused_computation.106 | convolution fusion | flops 303562752 | bytes 6685696 | tf_op jit(solution)/shard_map/kab,lab->kl/dot_general | solution.py:39
  108.1 10.6 %fusion.69 = f32[16,16]{1,0:T(8,128)S(1)} fusion(f32[16,256,384]{2,0,1:T(8,128)S(1)} %fusion.14, f32[16,256,384]{2,1,0:T(8,128)S(1)} %bitcast.144, f32[256,384]{1,0:T(8,128)S(1)} %fusion.83), kind=kOutput, calls=%fused_computation.105 | convolution fusion | flops 303562752 | bytes 12977152 | tf_op jit(solution)/shard_map/kab,lab->kl/dot_general | solution.py:39
  118.7 10.6 %fusion.66 = f32[16,16]{0,1:T(8,128)S(1)} fusion(f32[16,256,384]{2,0,1:T(8,128)S(1)} %fusion.14, f32[16,256,384]{2,1,0:T(8,128)S(1)} %bitcast.144, f32[256,384]{1,0:T(8,128)S(1)} %fusion.83), kind=kOutput, calls=%fused_computation.104 | convolution fusion | flops 303562752 | bytes 12977152 | tf_op jit(solution)/shard_map/kab,lab->kl/dot_general | solution.py:39
  129.2 45.8 %all-reduce.1 = (f32[16,16]{0,1:T(8,128)S(1)}, f32[16,16]{0,1:T(8,128)S(1)}, f32[16,16]{1,0:T(8,128)S(1)}, f32[16,16]{1,0:T(8,128)S(1)}) all-reduce(f32[16,16]{0,1:T(8,128)S(1)} %fusion.78, f32[16,16]{0,1:T(8,128)S(1)} %fusion.66, f32[16,16]{1,0:T(8,128)S(1)} %fusion.72, ...), channel_id=1, replica_groups=mesh['row'=4,'col'=8] {'row','col'}, use_global_device_ids=true, to_apply=%region_3.5 | all-reduce | flops 1024 | bytes 8192 | tf_op jit(solution)/shard_map/psum | solution.py:64
  183.6 13.2 %copy_subtract_fusion = f32[16,256,384]{2,0,1:T(8,128)} fusion(f32[16,256,384]{2,1,0:T(8,128)} %param.7, f32[16,256,384]{2,0,1:T(8,128)} %copy-done, f32[16,16]{1,0:T(8,128)S(1)} %fusion.111), kind=kOutput, calls=%fused_computation.80 | convolution fusion | flops 303562752 | bytes 18875392 | tf_op jit(solution)/shard_map/kab,kl->lab/dot_general | solution.py:43
  199.5 15.0 %broadcast_multiply_fusion.1 = (f32[16,256,384]{2,0,1:T(8,128)S(1)}, f32[16,256,384]{2,0,1:T(8,128)}) fusion(f32[256,384]{1,0:T(8,128)S(1)} %get-tuple-element.31, f32[16,16,1]{0,1,2:T(8,128)S(1)} %convolution_bitcast_fusion.4, f32[16,256,384]{2,1,0:T(8,128)} %param.7, f32[256,384]{1,0:T(8,128)S(1)} %fusion.83, f32[16,256,384]{2,0,1:T(8,128)} %copy_subtract_fusion), kind=kOutput, calls=%fused_computation.83 | convolution fusion | flops 308281344 | bytes 25953280 | tf_op jit(solution)/shard_map/kab,kl->lab/dot_general | solution.py:43
  218.9 3.7 collective-permute-done.6
  242.5 20.3 %fusion.31 = f32[16,256,384]{2,0,1:T(8,128)S(1)} fusion(f32[16,258,1]{2,0,1:T(8,128)} %copy.46, f32[16,1,384]{2,0,1:T(8,128)S(1)} %collective-permute-done.6, f32[16,256,384]{2,0,1:T(8,128)} %copy-done.4, f32[16,1,384]{2,0,1:T(8,128)S(1)} %collective-permute-done.7, f32[16,258,1]{2,0,1:T(8,128)} %copy.44, f32[16,256,384]{2,0,1:T(8,128)} %get-tuple-element.33, ...), kind=kLoop, calls=%fused_computation.43 | loop fusion | flops 31457280 | bytes 21709056 | tf_op jit(solution)/shard_map/add | solution.py:67
  262.9 8.1 %fusion.75 = f32[16,16]{1,0:T(8,128)S(1)} fusion(f32[16,256,384]{2,0,1:T(8,128)S(1)} %fusion.31, f32[256,384]{1,0:T(8,128)S(1)} %fusion.83), kind=kOutput, calls=%fused_computation.107 | convolution fusion | flops 303562752 | bytes 6685696 | tf_op jit(solution)/shard_map/kab,lab->kl/dot_general | solution.py:39
  271.1 8.3 %fusion.63 = f32[16,16]{1,0:T(8,128)S(1)} fusion(f32[16,256,384]{2,0,1:T(8,128)S(1)} %fusion.31, f32[16,256,384]{2,0,1:T(8,128)S(1)} %bitcast.150, f32[256,384]{1,0:T(8,128)S(1)} %fusion.83), kind=kOutput, calls=%fused_computation.103 | convolution fusion | flops 303562752 | bytes 12977152 | tf_op jit(solution)/shard_map/kab,lab->kl/dot_general | solution.py:39
  279.5 8.5 %convolution_bitcast_fusion.3 = f32[16,16]{0,1:T(8,128)S(1)} fusion(f32[16,256,384]{2,0,1:T(8,128)S(1)} %bitcast.148, f32[16,256,384]{2,0,1:T(8,128)S(1)} %fusion.31), kind=kOutput, calls=%fused_computation.112 | convolution fusion | flops 301989888 | bytes 12583936 | tf_op jit(solution)/shard_map/kab,lab->kl/dot_general | solution.py:39
  287.9 41.7 %all-reduce = (f32[16,16]{0,1:T(8,128)S(1)}, f32[16,16]{1,0:T(8,128)S(1)}, f32[16,16]{1,0:T(8,128)S(1)}) all-reduce(f32[16,16]{0,1:T(8,128)S(1)} %convolution_bitcast_fusion.3, f32[16,16]{1,0:T(8,128)S(1)} %fusion.75, f32[16,16]{1,0:T(8,128)S(1)} %fusion.63), channel_id=1, replica_groups=mesh['row'=4,'col'=8] {'row','col'}, use_global_device_ids=true, to_apply=%region_6.0 | all-reduce | flops 768 | bytes 6144 | tf_op jit(solution)/shard_map/psum | solution.py:71
  334.1 10.7 %convolution_subtract_fusion.1 = f32[16,256,384]{2,0,1:T(8,128)} fusion(f32[16,256,384]{2,0,1:T(8,128)} %copy_subtract_fusion, f32[16,256,384]{2,0,1:T(8,128)} %copy-done.1, f32[16,16]{1,0:T(8,128)S(1)} %fusion.100), kind=kOutput, calls=%fused_computation.93 | convolution fusion | flops 303562752 | bytes 18875392 | tf_op jit(solution)/shard_map/kab,kl->lab/dot_general | solution.py:43
  345.9 11.0 %broadcast_multiply_fusion = (f32[16,256,384]{2,0,1:T(8,128)S(1)}, f32[16,256,384]{2,0,1:T(8,128)}) fusion(f32[256,384]{1,0:T(8,128)S(1)} %get-tuple-element.31, f32[16,16,1]{0,1,2:T(8,128)S(1)} %convolution_bitcast_fusion.2, f32[16,256,384]{2,0,1:T(8,128)} %get-tuple-element.33, f32[16,256,384]{2,0,1:T(8,128)} %convolution_subtract_fusion.1, ...), kind=kOutput, calls=%fused_computation.82 | convolution fusion | flops 306708480 | bytes 25953280 | tf_op jit(solution)/shard_map/kab,kl->lab/dot_general | solution.py:43
  356.9 3.1 collective-permute-start.11
  361.5 4.2 collective-permute-done.10
  376.3 9.2 %fusion.98 = f32[16,256,384]{2,0,1:T(8,128)} fusion(f32[16,256,384]{2,0,1:T(8,128)} %get-tuple-element.33, f32[16,16]{1,0:T(8,128)S(1)} %fusion.100), kind=kOutput, calls=%fused_computation.144 | convolution fusion | flops 301989888 | bytes 12583936 | tf_op jit(solution)/shard_map/kab,kl->lab/dot_general | solution.py:43
  390.6 19.7 %fusion.21 = f32[16,256,384]{2,0,1:T(8,128)S(1)} fusion(f32[16,258,1]{2,0,1:T(8,128)} %copy.57, f32[16,1,384]{2,0,1:T(8,128)S(1)} %collective-permute-done.10, f32[16,256,384]{2,0,1:T(8,128)} %copy-done.3, f32[16,1,384]{2,0,1:T(8,128)S(1)} %collective-permute-done.11, f32[16,258,1]{2,0,1:T(8,128)} %copy.55, f32[16,256,384]{2,0,1:T(8,128)} %get-tuple-element.35, ...), kind=kLoop, calls=%fused_computation.25 | loop fusion | flops 31457280 | bytes 21709056 | tf_op jit(solution)/shard_map/add | solution.py:67
  413.0 10.2 %convolution_bitcast_fusion.1 = f32[16,16]{0,1:T(8,128)S(1)} fusion(f32[16,256,384]{2,0,1:T(8,128)} %get-tuple-element.35, f32[16,256,384]{2,0,1:T(8,128)S(1)} %fusion.21), kind=kOutput, calls=%fused_computation.109 | convolution fusion | flops 301989888 | bytes 12583936 | tf_op jit(solution)/shard_map/kab,lab->kl/dot_general | solution.py:39
  423.2 43.2 %psum.63 = f32[16,16]{0,1:T(8,128)S(1)} all-reduce(f32[16,16]{0,1:T(8,128)S(1)} %convolution_bitcast_fusion.1), channel_id=1, replica_groups=mesh['row'=4,'col'=8] {'row','col'}, use_global_device_ids=true, to_apply=%region_9.12 | all-reduce | flops 256 | bytes 2048 | tf_op jit(solution)/shard_map/psum | solution.py:71
  470.9 8.9 %convolution_subtract_fusion = f32[16,256,384]{2,0,1:T(8,128)S(1)} fusion(f32[16,256,384]{2,0,1:T(8,128)} %convolution_subtract_fusion.1, f32[16,16,1]{0,1,2:T(8,128)S(1)} %convolution_bitcast_fusion, f32[16,256,384]{2,0,1:T(8,128)} %copy-done.5), kind=kOutput, calls=%fused_computation.92 | convolution fusion | flops 303562752 | bytes 18875392 | tf_op jit(solution)/shard_map/kab,kl->lab/dot_general | solution.py:43
  479.9 7.6 %fusion.123 = f32[16,256,384]{2,0,1:T(8,128)S(1)} fusion(f32[16,16,1]{0,1,2:T(8,128)S(1)} %convolution_bitcast_fusion, f32[16,256,384]{2,0,1:T(8,128)} %get-tuple-element.35), kind=kOutput, calls=%fused_computation.185 | convolution fusion | flops 301989888 | bytes 12583936 | tf_op jit(solution)/shard_map/kab,kl->lab/dot_general | solution.py:43
  487.5 12.1 %add_add_fusion = f32[16,256,384]{2,0,1:T(8,128)S(1)} fusion(f32[16,256,384]{2,0,1:T(8,128)S(1)} %fusion.123, f32[16,256,384]{2,0,1:T(8,128)} %fusion.98, f32[16,256,384]{2,1,0:T(8,128)S(1)} %bitcast.146, f32[256,384]{1,0:T(8,128)S(1)} %fusion.83, f32[16,16]{1,0:T(8,128)S(1)} %fusion.111), kind=kOutput, calls=%fused_computation.72 | convolution fusion | flops 306708480 | bytes 25560064 | tf_op jit(solution)/shard_map/kab,kl->lab/dot_general | solution.py:43
  499.6 4.6 copy.62
  504.3 4.6 copy.63
  (142 shorter events, 90.2 us)
Async XLA Ops:
  1.3 8.4 %collective-permute-start = (f32[1,384]{1,0:T(1,128)S(1)}, f32[1,384]{1,0:T(1,128)S(1)}, u32[]{:S(2)}, u32[]{:S(2)}) collective-permute-start(f32[1,384]{1,0:T(1,128)S(1)} %slice.108), channel_id=1, source_target_pairs={{0,8},{8,16},{16,24},{1,9},{9,17},{17,25},{2,10},{10,18},{18,26},{... | collective-permute-start | bytes 4616 | tf_op jit(solution)/shard_map/ppermute | solution.py:13
  7.3 2.4 collective-permute-start.1
  13.6 11.7 %copy-start.12 = (s32[256,384]{1,0:T(8,128)S(1)}, s32[256,384]{1,0:T(8,128)}, u32[]{:S(2)}) copy-start(s32[256,384]{1,0:T(8,128)} %param.10) | copy-start | bytes 1179652
  20.5 9.2 %copy-start.2 = (f32[16,256,384]{2,0,1:T(8,128)}, f32[16,256,384]{2,0,1:T(8,128)S(1)}, u32[]{:S(2)}) copy-start(f32[16,256,384]{2,0,1:T(8,128)S(1)} %multiply_multiply_fusion) | copy-start | bytes 18874372
  20.5 5.6 %collective-permute-start.3 = (f32[16,1,384]{2,0,1:T(8,128)S(1)}, f32[16,1,384]{2,0,1:T(8,128)S(1)}, u32[]{:S(2)}, u32[]{:S(2)}) collective-permute-start(f32[16,1,384]{2,0,1:T(8,128)S(1)} %get-tuple-element.29), channel_id=1, source_target_pairs={{0,8},{8,16},{16,24},{1,9},{9,17},{17,25},{2,10},{10,18},{18,26},{... | collective-permute-start | bytes 73736 | tf_op jit(solution)/shard_map/ppermute | solution.py:24
  24.0 5.7 %collective-permute-start.2 = (f32[16,1,384]{2,0,1:T(8,128)S(1)}, f32[16,1,384]{2,0,1:T(8,128)S(1)}, u32[]{:S(2)}, u32[]{:S(2)}) collective-permute-start(f32[16,1,384]{2,0,1:T(8,128)S(1)} %get-tuple-element.30), channel_id=1, source_target_pairs={{8,0},{16,8},{24,16},{9,1},{17,9},{25,17},{10,2},{18,10},{26,18},{... | collective-permute-start | bytes 73736 | tf_op jit(solution)/shard_map/ppermute | solution.py:26
  37.6 41.1 %copy-start.6 = (f32[256,384]{1,0:T(8,128)S(1)}, f32[256,384]{1,0:T(8,128)}, u32[]{:S(2)}) copy-start(f32[256,384]{1,0:T(8,128)} %param.9) | copy-start | bytes 1179652
  37.6 38.6 %collective-permute-start.5 = (f32[16,258,1]{1,0,2:T(8,128)S(1)}, f32[16,258,1]{1,0,2:T(8,128)S(1)}, u32[]{:S(2)}, u32[]{:S(2)}) collective-permute-start(f32[16,258,1]{1,0,2:T(8,128)S(1)} %copy.32), channel_id=1, source_target_pairs={{0,1},{1,2},{2,3},{3,4},{4,5},{5,6},{6,7},{8,9},{9,10},{10,11},{11... | collective-permute-start | bytes 49544 | tf_op jit(solution)/shard_map/ppermute | solution.py:24
  41.3 32.4 %collective-permute-start.4 = (f32[16,258,1]{1,0,2:T(8,128)S(1)}, f32[16,258,1]{1,0,2:T(8,128)S(1)}, u32[]{:S(2)}, u32[]{:S(2)}) collective-permute-start(f32[16,258,1]{1,0,2:T(8,128)S(1)} %copy.30), channel_id=1, source_target_pairs={{1,0},{2,1},{3,2},{4,3},{5,4},{6,5},{7,6},{9,8},{10,9},{11,10},{12... | collective-permute-start | bytes 49544 | tf_op jit(solution)/shard_map/ppermute | solution.py:26
  76.2 31.8 %slice-start = ((s8[6291456]{0:T(1024)(128)(4,1)}), s8[2097152]{0:T(1024)(128)(4,1)S(1)}, s32[]{:S(2)}) async-start(s8[6291456]{0:T(1024)(128)(4,1)} %bitcast.143), calls=%async_computation | async-start | bytes 4194304
  78.7 29.3 %slice-start.1 = ((s8[6291456]{0:T(1024)(128)(4,1)}), s8[4194304]{0:T(1024)(128)(4,1)S(1)}, s32[]{:S(2)}) async-start(s8[6291456]{0:T(1024)(128)(4,1)} %bitcast.143), calls=%async_computation.1 | async-start | bytes 8388608
  99.9 18.8 %copy-start = (f32[16,256,384]{2,0,1:T(8,128)}, f32[16,256,384]{2,0,1:T(8,128)S(1)}, u32[]{:S(2)}) copy-start(f32[16,256,384]{2,0,1:T(8,128)S(1)} %fusion.14) | copy-start | bytes 18874372
  214.5 4.3 collective-permute-start.7
  216.9 5.7 %collective-permute-start.6 = (f32[16,1,384]{2,0,1:T(8,128)S(1)}, f32[16,1,384]{2,0,1:T(8,128)S(1)}, u32[]{:S(2)}, u32[]{:S(2)}) collective-permute-start(f32[16,1,384]{2,0,1:T(8,128)S(1)} %get-tuple-element.28), channel_id=1, source_target_pairs={{8,0},{16,8},{24,16},{9,1},{17,9},{25,17},{10,2},{18,10},{26,18},{... | collective-permute-start | bytes 73736 | tf_op jit(solution)/shard_map/ppermute | solution.py:26
  230.5 9.5 %collective-permute-start.9 = (f32[16,258,1]{1,0,2:T(8,128)S(1)}, f32[16,258,1]{1,0,2:T(8,128)S(1)}, u32[]{:S(2)}, u32[]{:S(2)}) collective-permute-start(f32[16,258,1]{1,0,2:T(8,128)S(1)} %copy.45), channel_id=1, source_target_pairs={{0,1},{1,2},{2,3},{3,4},{4,5},{5,6},{6,7},{8,9},{9,10},{10,11},{11... | collective-permute-start | bytes 49544 | tf_op jit(solution)/shard_map/ppermute | solution.py:24
  231.8 5.6 %collective-permute-start.8 = (f32[16,258,1]{1,0,2:T(8,128)S(1)}, f32[16,258,1]{1,0,2:T(8,128)S(1)}, u32[]{:S(2)}, u32[]{:S(2)}) collective-permute-start(f32[16,258,1]{1,0,2:T(8,128)S(1)} %copy.43), channel_id=1, source_target_pairs={{1,0},{2,1},{3,2},{4,3},{5,4},{6,5},{7,6},{9,8},{10,9},{11,10},{12... | collective-permute-start | bytes 49544 | tf_op jit(solution)/shard_map/ppermute | solution.py:26
  240.0 31.1 %slice-start.6 = ((s8[6291456]{0:T(1024)(128)(4,1)}), s8[2097152]{0:T(1024)(128)(4,1)S(1)}, s32[]{:S(2)}) async-start(s8[6291456]{0:T(1024)(128)(4,1)} %bitcast.149), calls=%async_computation.6 | async-start | bytes 4194304
  242.5 28.5 %slice-start.7 = ((s8[6291456]{0:T(1024)(128)(4,1)}), s8[4194304]{0:T(1024)(128)(4,1)S(1)}, s32[]{:S(2)}) async-start(s8[6291456]{0:T(1024)(128)(4,1)} %bitcast.149), calls=%async_computation.7 | async-start | bytes 8388608
  262.9 16.6 %copy-start.1 = (f32[16,256,384]{2,0,1:T(8,128)}, f32[16,256,384]{2,0,1:T(8,128)S(1)}, u32[]{:S(2)}) copy-start(f32[16,256,384]{2,0,1:T(8,128)S(1)} %fusion.31) | copy-start | bytes 18874372
  262.9 16.6 %slice-start.4 = ((s8[6291456]{0:T(1024)(128)(4,1)}), s8[4194304]{0:T(1024)(128)(4,1)S(1)}, s32[]{:S(2)}) async-start(s8[6291456]{0:T(1024)(128)(4,1)} %bitcast.147), calls=%async_computation.4 | async-start | bytes 8388608
  356.8 8.8 %copy-start.3 = (f32[16,256,384]{2,0,1:T(8,128)}, f32[16,256,384]{2,0,1:T(8,128)S(1)}, u32[]{:S(2)}) copy-start(f32[16,256,384]{2,0,1:T(8,128)S(1)} %get-tuple-element.34) | copy-start | bytes 18874372
  356.9 4.6 collective-permute-start.11
  359.9 5.7 %collective-permute-start.10 = (f32[16,1,384]{2,0,1:T(8,128)S(1)}, f32[16,1,384]{2,0,1:T(8,128)S(1)}, u32[]{:S(2)}, u32[]{:S(2)}) collective-permute-start(f32[16,1,384]{2,0,1:T(8,128)S(1)} %get-tuple-element.26), channel_id=1, source_target_pairs={{8,0},{16,8},{24,16},{9,1},{17,9},{25,17},{10,2},{18,10},{26,18},{... | collective-permute-start | bytes 73736 | tf_op jit(solution)/shard_map/ppermute | solution.py:26
  373.6 17.0 %copy-start.7 = (f32[256,384]{1,0:T(8,128)S(1)}, f32[256,384]{1,0:T(8,128)}, u32[]{:S(2)}) copy-start(f32[256,384]{1,0:T(8,128)} %param.8) | copy-start | bytes 1179652
  373.6 17.0 %copy-start.8 = (f32[256,384]{1,0:T(8,128)S(1)}, f32[256,384]{1,0:T(8,128)}, u32[]{:S(2)}) copy-start(f32[256,384]{1,0:T(8,128)} %get-tuple-element.15) | copy-start | bytes 1179652
  373.6 17.0 %copy-start.9 = (f32[256,384]{1,0:T(8,128)S(1)}, f32[256,384]{1,0:T(8,128)}, u32[]{:S(2)}) copy-start(f32[256,384]{1,0:T(8,128)} %get-tuple-element.17) | copy-start | bytes 1179652
  373.6 17.0 %copy-start.10 = (f32[256,384]{1,0:T(8,128)S(1)}, f32[256,384]{1,0:T(8,128)}, u32[]{:S(2)}) copy-start(f32[256,384]{1,0:T(8,128)} %get-tuple-element.18) | copy-start | bytes 1179652
  373.6 17.0 %copy-start.11 = (f32[256,384]{1,0:T(8,128)S(1)}, f32[256,384]{1,0:T(8,128)}, u32[]{:S(2)}) copy-start(f32[256,384]{1,0:T(8,128)} %convert_element_type.3) | copy-start | bytes 1179652
  373.6 14.4 %collective-permute-start.13 = (f32[16,258,1]{1,0,2:T(8,128)S(1)}, f32[16,258,1]{1,0,2:T(8,128)S(1)}, u32[]{:S(2)}, u32[]{:S(2)}) collective-permute-start(f32[16,258,1]{1,0,2:T(8,128)S(1)} %copy.56), channel_id=1, source_target_pairs={{0,1},{1,2},{2,3},{3,4},{4,5},{5,6},{6,7},{8,9},{9,10},{10,11},{11... | collective-permute-start | bytes 49544 | tf_op jit(solution)/shard_map/ppermute | solution.py:24
  375.0 10.5 %collective-permute-start.12 = (f32[16,258,1]{1,0,2:T(8,128)S(1)}, f32[16,258,1]{1,0,2:T(8,128)S(1)}, u32[]{:S(2)}, u32[]{:S(2)}) collective-permute-start(f32[16,258,1]{1,0,2:T(8,128)S(1)} %copy.54), channel_id=1, source_target_pairs={{1,0},{2,1},{3,2},{4,3},{5,4},{6,5},{7,6},{9,8},{10,9},{11,10},{12... | collective-permute-start | bytes 49544 | tf_op jit(solution)/shard_map/ppermute | solution.py:26
  413.0 74.5 %slice-start.2 = ((s8[6291456]{0:T(1024)(128)(4,1)}), s8[2097152]{0:T(1024)(128)(4,1)S(1)}, s32[]{:S(2)}) async-start(s8[6291456]{0:T(1024)(128)(4,1)} %bitcast.145), calls=%async_computation.2 | async-start | bytes 4194304
  470.9 16.6 %slice-start.3 = ((s8[6291456]{0:T(1024)(128)(4,1)}), s8[4194304]{0:T(1024)(128)(4,1)S(1)}, s32[]{:S(2)}) async-start(s8[6291456]{0:T(1024)(128)(4,1)} %bitcast.145), calls=%async_computation.3 | async-start | bytes 8388608
  (3 other events, 19.2 us)
where the time goes:
time: 516 us; the launch traced here: 509 us
  matrix products  186 us (36%)
  blocking collectives  131 us (25%)
  other arithmetic  101 us (20%)
  local copies, waits for them, and re-layouts  45.3 us (9%)
  starting transfers between devices  30 us (6%)
  waiting for transfers between devices  15 us (3%)
    dot_general x8, matrix products, gram(): return jnp.einsum('kab,lab->kl', left, right, precision=exact_precision)  95.2 us
    dot_general x8, matrix products, combine(): return jnp.einsum('kab,kl->lab', field, matrix, precision=exact_precision)  87.7 us
    psum x2, blocking collectives, shards(): lax.psum((gram(direction, image), gram(image, precond), gram(image, weigh...  84.9 us
    add x3, other arithmetic, shards(): pad_nodes * direction  61.2 us
    psum x1, blocking collectives, shards(): gram_now = lax.psum(gram(residual, precond), ('row', 'col'))  45.8 us
    ppermute x6, starting transfers between devices, extended(): lax.ppermute(tail, axis, [(i, (i + 1) % count) for i in range(ends)])  15.2 us
    ppermute x6, waiting for transfers between devices, extended(): lax.ppermute(head, axis, [((i + 1) % count, i) for i in range(ends)])  14 us
    unnamed x44, local copies, waits for them, and re-layouts  12.1 us
  transfers between devices with their start and end apart: 14, of which 5 were waited for; matrix products, arithmetic and copies ran while one was open for 10% of the time, Pallas kernels for 0%

commit v1 on v0

--- a/solution.py
+++ b/solution.py
@@ -5,6 +5,11 @@
 
 ITERS = 3
 exact_precision = lax.Precision.HIGHEST
+
+
+def axis_by_axis(x, inner_axis, outer_axis):
+    inner = lax.psum(x, inner_axis)
+    return lax.psum(inner, outer_axis)
 
 
 def passed_along(shard, axis, by):
@@ -68,8 +73,8 @@
             diagonal * direction - neighbour_sum(padded, cond_x, cond_above, cond_y, cond_left)
         )
         weighted = image * inverse
-        curvature, cross_term, image_term = lax.psum(
-            (gram(direction, image), gram(image, precond), gram(image, weighted)), ("row", "col")
+        curvature, cross_term, image_term = axis_by_axis(
+            (gram(direction, image), gram(image, precond), gram(image, weighted)), "col", "row"
         )
         alpha_block = small_solve(curvature, gram_now)
         solution = solution + combine(direction, alpha_block)

time: 516 us -> 518 us (level)
  blocking collectives: 131 us -> 156 us
  matrix products: 186 us -> 165 us
  starting transfers between devices: 30 us -> 23.6 us
    psum x2 -> x6, blocking collectives: 84.9 us -> 113 us  [the longest x3 67.5 us: axis_by_axis(): inner = lax.psum(x, inner_axis)]
    dot_general x8, matrix products: 95.2 us -> 74.5 us  [gram(): return jnp.einsum('kab,lab->kl', left, right, precision=exact_precision)]
    ppermute x6, starting transfers between devices: 15.2 us -> 8.74 us  [extended(): lax.ppermute(tail, axis, [(i, (i + 1) % count) for i in range(ends)])]
  transfers between devices with their start and end apart: 14 -> 14, of which waited for: 5 -> 5; matrix products, arithmetic and copies ran while one was open for 10% -> 5% of each run, Pallas kernels for 0% -> 0%
where the time goes in v1:
time: 518 us; the launch traced here: 508 us
  matrix products  165 us (32%)
  blocking collectives  156 us (30%)
  other arithmetic  101 us (19%)
  local copies, waits for them, and re-layouts  45.4 us (9%)
  starting transfers between devices  23.6 us (5%)
  waiting for transfers between devices  15 us (3%)
    dot_general x8, matrix products, combine(): return jnp.einsum('kab,kl->lab', field, matrix, precision=exact_precision)  87.7 us
    dot_general x8, matrix products, gram(): return jnp.einsum('kab,lab->kl', left, right, precision=exact_precision)  74.5 us
    psum x3, blocking collectives, axis_by_axis(): inner = lax.psum(x, inner_axis)  67.5 us
    add x3, other arithmetic, shards(): pad_nodes * direction  60.6 us
    psum x3, blocking collectives, axis_by_axis(): return lax.psum(inner, outer_axis)  45.3 us
    psum x1, blocking collectives, shards(): gram_now = lax.psum(gram(residual, precond), ('row', 'col'))  43.7 us
    ppermute x6, waiting for transfers between devices, extended(): lax.ppermute(head, axis, [((i + 1) % count, i) for i in range(ends)])  14.9 us
    unnamed x44, local copies, waits for them, and re-layouts  12.1 us
  transfers between devices with their start and end apart: 14, of which 5 were waited for; matrix products, arithmetic and copies ran while one was open for 5% of the time, Pallas kernels for 0%

profile of v1, /device:TPU:0, one launch (start us, length us, event | category | flops | bytes accessed | tf_op | source)
XLA Modules:
  0.0 508.5 jit_solution(15997526571833877776)
XLA Ops:
  1.5 5.2 %collective-permute-start = (f32[1,384]{1,0:T(1,128)S(1)}, f32[1,384]{1,0:T(1,128)S(1)}, u32[]{:S(2)}, u32[]{:S(2)}) collective-permute-start(f32[1,384]{1,0:T(1,128)S(1)} %slice.108), channel_id=1, source_target_pairs={{0,8},{8,16},{16,24},{1,9},{9,17},{17,25},{2,10},{10,18},{18,26},{... | collective-permute-start | bytes 4616 | tf_op jit(solution)/shard_map/ppermute | solution.py:18
  14.8 10.1 %fusion.78 = f32[16,16]{0,1:T(8,128)S(1)} fusion(f32[16,256,384]{2,1,0:T(8,128)S(1)} %copy-done, f32[256,384]{1,0:T(8,128)S(1)} %fusion.83), kind=kOutput, calls=%fused_computation.115 | convolution fusion | flops 303562752 | bytes 6685696 | tf_op jit(solution)/shard_map/kab,lab->kl/dot_general | solution.py:44
  25.0 43.7 %psum.107 = f32[16,16]{0,1:T(8,128)S(1)} all-reduce(f32[16,16]{0,1:T(8,128)S(1)} %fusion.78), channel_id=1, replica_groups=mesh['row'=4,'col'=8] {'row','col'}, use_global_device_ids=true, to_apply=%region_4.6 | all-reduce | flops 256 | bytes 2048 | tf_op jit(solution)/shard_map/psum | solution.py:69
  70.2 6.8 %multiply_multiply_fusion = f32[16,256,384]{2,0,1:T(8,128)S(1)} fusion(f32[16,256,384]{2,1,0:T(8,128)} %param.7, f32[256,384]{1,0:T(8,128)S(1)} %get-tuple-element.36, f32[256,384]{1,0:T(8,128)S(1)} %fusion.83), kind=kLoop, calls=%fused_computation.14 | loop fusion | flops 3145728 | bytes 13369344 | tf_op jit(solution)/shard_map/mul | solution.py:71
  81.2 3.7 collective-permute-done.2
  104.9 21.5 %fusion.14 = f32[16,256,384]{2,0,1:T(8,128)S(1)} fusion(f32[16,258,1]{2,0,1:T(8,128)} %copy.33, f32[16,1,384]{2,0,1:T(8,128)S(1)} %collective-permute-done.2, f32[16,256,384]{2,0,1:T(8,128)} %copy-done.3, f32[16,1,384]{2,0,1:T(8,128)S(1)} %collective-permute-done.3, f32[16,258,1]{2,0,1:T(8,128)} %copy.31, f32[16,256,384]{2,1,0:T(8,128)} %param.7, ...), kind=kLoop, calls=%fused_computation.17 | loop fusion | flops 33030144 | bytes 22102272 | tf_op jit(solution)/shard_map/add | solution.py:72
  126.5 8.1 %fusion.72 = f32[16,16]{1,0:T(8,128)S(1)} fusion(f32[16,256,384]{2,0,1:T(8,128)S(1)} %fusion.14, f32[256,384]{1,0:T(8,128)S(1)} %fusion.83), kind=kOutput, calls=%fused_computation.106 | convolution fusion | flops 303562752 | bytes 6685696 | tf_op jit(solution)/shard_map/kab,lab->kl/dot_general | solution.py:44
  134.6 10.4 %fusion.69 = f32[16,16]{1,0:T(8,128)S(1)} fusion(f32[16,256,384]{2,0,1:T(8,128)S(1)} %fusion.14, f32[16,256,384]{2,1,0:T(8,128)S(1)} %bitcast.144, f32[256,384]{1,0:T(8,128)S(1)} %fusion.83), kind=kOutput, calls=%fused_computation.105 | convolution fusion | flops 303562752 | bytes 12977152 | tf_op jit(solution)/shard_map/kab,lab->kl/dot_general | solution.py:44
  145.0 10.6 %fusion.66 = f32[16,16]{0,1:T(8,128)S(1)} fusion(f32[16,256,384]{2,0,1:T(8,128)S(1)} %fusion.14, f32[16,256,384]{2,1,0:T(8,128)S(1)} %bitcast.144, f32[256,384]{1,0:T(8,128)S(1)} %fusion.83), kind=kOutput, calls=%fused_computation.104 | convolution fusion | flops 303562752 | bytes 12977152 | tf_op jit(solution)/shard_map/kab,lab->kl/dot_general | solution.py:44
  155.6 25.3 %all-reduce.1 = (f32[16,16]{0,1:T(8,128)S(1)}, f32[16,16]{1,0:T(8,128)S(1)}, f32[16,16]{1,0:T(8,128)S(1)}) all-reduce(f32[16,16]{0,1:T(8,128)S(1)} %fusion.66, f32[16,16]{1,0:T(8,128)S(1)} %fusion.72, f32[16,16]{1,0:T(8,128)S(1)} %fusion.69), channel_id=1, replica_groups=mesh['row'=4,'col'=8] {'col'}, use_global_device_ids=true, to_apply=%region_0.0 | all-reduce | flops 768 | bytes 6144 | tf_op jit(solution)/shard_map/psum | solution.py:11
  180.9 17.3 %all-reduce.3 = (f32[16,16]{0,1:T(8,128)S(1)}, f32[16,16]{1,0:T(8,128)S(1)}, f32[16,16]{1,0:T(8,128)S(1)}) all-reduce(f32[16,16]{0,1:T(8,128)S(1)} %get-tuple-element.11, f32[16,16]{1,0:T(8,128)S(1)} %get-tuple-element.12, f32[16,16]{1,0:T(8,128)S(1)} %get-tuple-element.13), channel_id=1, replica_groups=mesh['row'=4,'col'=8] {'row'}, use_global_device_ids=true, to_apply=%region_1.0 | all-reduce | flops 768 | bytes 6144 | tf_op jit(solution)/shard_map/psum | solution.py:12
  202.6 13.2 %copy_subtract_fusion = f32[16,256,384]{2,0,1:T(8,128)} fusion(f32[16,256,384]{2,1,0:T(8,128)} %param.7, f32[16,256,384]{2,0,1:T(8,128)} %copy-done.2, f32[16,16]{1,0:T(8,128)S(1)} %fusion.111), kind=kOutput, calls=%fused_computation.80 | convolution fusion | flops 303562752 | bytes 18875392 | tf_op jit(solution)/shard_map/kab,kl->lab/dot_general | solution.py:48
  218.5 15.0 %broadcast_multiply_fusion.1 = (f32[16,256,384]{2,0,1:T(8,128)S(1)}, f32[16,256,384]{2,0,1:T(8,128)}) fusion(f32[256,384]{1,0:T(8,128)S(1)} %get-tuple-element.36, f32[16,16,1]{0,1,2:T(8,128)S(1)} %convolution_bitcast_fusion.4, f32[16,256,384]{2,1,0:T(8,128)} %param.7, f32[256,384]{1,0:T(8,128)S(1)} %fusion.83, f32[16,256,384]{2,0,1:T(8,128)} %copy_subtract_fusion), kind=kOutput, calls=%fused_computation.83 | convolution fusion | flops 308281344 | bytes 25953280 | tf_op jit(solution)/shard_map/kab,kl->lab/dot_general | solution.py:48
  259.2 19.8 %fusion.31 = f32[16,256,384]{2,0,1:T(8,128)S(1)} fusion(f32[16,258,1]{2,0,1:T(8,128)} %copy.46, f32[16,1,384]{2,0,1:T(8,128)S(1)} %collective-permute-done.6, f32[16,256,384]{2,0,1:T(8,128)} %copy-done.5, f32[16,1,384]{2,0,1:T(8,128)S(1)} %collective-permute-done.7, f32[16,258,1]{2,0,1:T(8,128)} %copy.44, f32[16,256,384]{2,0,1:T(8,128)} %get-tuple-element.38, ...), kind=kLoop, calls=%fused_computation.43 | loop fusion | flops 31457280 | bytes 21709056 | tf_op jit(solution)/shard_map/add | solution.py:72
  279.0 8.1 %fusion.75 = f32[16,16]{1,0:T(8,128)S(1)} fusion(f32[16,256,384]{2,0,1:T(8,128)S(1)} %fusion.31, f32[256,384]{1,0:T(8,128)S(1)} %fusion.83), kind=kOutput, calls=%fused_computation.107 | convolution fusion | flops 303562752 | bytes 6685696 | tf_op jit(solution)/shard_map/kab,lab->kl/dot_general | solution.py:44
  287.2 8.3 %fusion.63 = f32[16,16]{1,0:T(8,128)S(1)} fusion(f32[16,256,384]{2,0,1:T(8,128)S(1)} %fusion.31, f32[16,256,384]{2,0,1:T(8,128)S(1)} %bitcast.150, f32[256,384]{1,0:T(8,128)S(1)} %fusion.83), kind=kOutput, calls=%fused_computation.103 | convolution fusion | flops 303562752 | bytes 12977152 | tf_op jit(solution)/shard_map/kab,lab->kl/dot_general | solution.py:44
  295.6 8.6 %convolution_bitcast_fusion.3 = f32[16,16]{0,1:T(8,128)S(1)} fusion(f32[16,256,384]{2,0,1:T(8,128)S(1)} %bitcast.148, f32[16,256,384]{2,0,1:T(8,128)S(1)} %fusion.31), kind=kOutput, calls=%fused_computation.112 | convolution fusion | flops 301989888 | bytes 12583936 | tf_op jit(solution)/shard_map/kab,lab->kl/dot_general | solution.py:44
  304.2 26.3 %all-reduce = (f32[16,16]{0,1:T(8,128)S(1)}, f32[16,16]{1,0:T(8,128)S(1)}, f32[16,16]{1,0:T(8,128)S(1)}) all-reduce(f32[16,16]{0,1:T(8,128)S(1)} %convolution_bitcast_fusion.3, f32[16,16]{1,0:T(8,128)S(1)} %fusion.75, f32[16,16]{1,0:T(8,128)S(1)} %fusion.63), channel_id=1, replica_groups=mesh['row'=4,'col'=8] {'col'}, use_global_device_ids=true, to_apply=%region_9.0 | all-reduce | flops 768 | bytes 6144 | tf_op jit(solution)/shard_map/psum | solution.py:11
  330.4 17.5 %all-reduce.2 = (f32[16,16]{0,1:T(8,128)S(1)}, f32[16,16]{1,0:T(8,128)S(1)}, f32[16,16]{1,0:T(8,128)S(1)}) all-reduce(f32[16,16]{0,1:T(8,128)S(1)} %get-tuple-element.8, f32[16,16]{1,0:T(8,128)S(1)} %get-tuple-element.9, f32[16,16]{1,0:T(8,128)S(1)} %get-tuple-element.10), channel_id=1, replica_groups=mesh['row'=4,'col'=8] {'row'}, use_global_device_ids=true, to_apply=%region_10.0 | all-reduce | flops 768 | bytes 6144 | tf_op jit(solution)/shard_map/psum | solution.py:12
  352.4 10.7 %convolution_subtract_fusion.1 = f32[16,256,384]{2,0,1:T(8,128)} fusion(f32[16,256,384]{2,0,1:T(8,128)} %copy_subtract_fusion, f32[16,256,384]{2,0,1:T(8,128)} %copy-done.1, f32[16,16]{1,0:T(8,128)S(1)} %fusion.100), kind=kOutput, calls=%fused_computation.93 | convolution fusion | flops 303562752 | bytes 18875392 | tf_op jit(solution)/shard_map/kab,kl->lab/dot_general | solution.py:48
  364.2 11.0 %broadcast_multiply_fusion = (f32[16,256,384]{2,0,1:T(8,128)S(1)}, f32[16,256,384]{2,0,1:T(8,128)}) fusion(f32[256,384]{1,0:T(8,128)S(1)} %get-tuple-element.36, f32[16,16,1]{0,1,2:T(8,128)S(1)} %convolution_bitcast_fusion.2, f32[16,256,384]{2,0,1:T(8,128)} %get-tuple-element.38, f32[16,256,384]{2,0,1:T(8,128)} %convolution_subtract_fusion.1, ...), kind=kOutput, calls=%fused_computation.82 | convolution fusion | flops 306708480 | bytes 25953280 | tf_op jit(solution)/shard_map/kab,kl->lab/dot_general | solution.py:48
  378.2 4.0 collective-permute-done.10
  392.8 9.1 %fusion.98 = f32[16,256,384]{2,0,1:T(8,128)} fusion(f32[16,256,384]{2,0,1:T(8,128)} %get-tuple-element.38, f32[16,16]{1,0:T(8,128)S(1)} %fusion.100), kind=kOutput, calls=%fused_computation.144 | convolution fusion | flops 301989888 | bytes 12583936 | tf_op jit(solution)/shard_map/kab,kl->lab/dot_general | solution.py:48
  407.0 19.3 %fusion.21 = f32[16,256,384]{2,0,1:T(8,128)S(1)} fusion(f32[16,258,1]{2,0,1:T(8,128)} %copy.57, f32[16,1,384]{2,0,1:T(8,128)S(1)} %collective-permute-done.10, f32[16,256,384]{2,0,1:T(8,128)} %copy-done.4, f32[16,1,384]{2,0,1:T(8,128)S(1)} %collective-permute-done.11, f32[16,258,1]{2,0,1:T(8,128)} %copy.55, f32[16,256,384]{2,0,1:T(8,128)} %get-tuple-element.40, ...), kind=kLoop, calls=%fused_computation.25 | loop fusion | flops 31457280 | bytes 21709056 | tf_op jit(solution)/shard_map/add | solution.py:72
  429.1 10.2 %convolution_bitcast_fusion.1 = f32[16,16]{0,1:T(8,128)S(1)} fusion(f32[16,256,384]{2,0,1:T(8,128)} %get-tuple-element.40, f32[16,256,384]{2,0,1:T(8,128)S(1)} %fusion.21), kind=kOutput, calls=%fused_computation.109 | convolution fusion | flops 301989888 | bytes 12583936 | tf_op jit(solution)/shard_map/kab,lab->kl/dot_general | solution.py:44
  439.3 15.9 %psum.118 = f32[16,16]{0,1:T(8,128)S(1)} all-reduce(f32[16,16]{0,1:T(8,128)S(1)} %convolution_bitcast_fusion.1), channel_id=1, replica_groups=mesh['row'=4,'col'=8] {'col'}, use_global_device_ids=true, to_apply=%region_15.18 | all-reduce | flops 256 | bytes 2048 | tf_op jit(solution)/shard_map/psum | solution.py:11
  455.2 10.5 %psum.119 = f32[16,16]{0,1:T(8,128)S(1)} all-reduce(f32[16,16]{0,1:T(8,128)S(1)} %psum.118), channel_id=1, replica_groups=mesh['row'=4,'col'=8] {'row'}, use_global_device_ids=true, to_apply=%region_16.19 | all-reduce | flops 256 | bytes 2048 | tf_op jit(solution)/shard_map/psum | solution.py:12
  470.3 8.9 %convolution_subtract_fusion = f32[16,256,384]{2,0,1:T(8,128)S(1)} fusion(f32[16,256,384]{2,0,1:T(8,128)} %convolution_subtract_fusion.1, f32[16,16,1]{0,1,2:T(8,128)S(1)} %convolution_bitcast_fusion, f32[16,256,384]{2,0,1:T(8,128)} %copy-done.6), kind=kOutput, calls=%fused_computation.92 | convolution fusion | flops 303562752 | bytes 18875392 | tf_op jit(solution)/shard_map/kab,kl->lab/dot_general | solution.py:48
  479.2 7.6 %fusion.123 = f32[16,256,384]{2,0,1:T(8,128)S(1)} fusion(f32[16,16,1]{0,1,2:T(8,128)S(1)} %convolution_bitcast_fusion, f32[16,256,384]{2,0,1:T(8,128)} %get-tuple-element.40), kind=kOutput, calls=%fused_computation.185 | convolution fusion | flops 301989888 | bytes 12583936 | tf_op jit(solution)/shard_map/kab,kl->lab/dot_general | solution.py:48
  486.9 12.1 %add_add_fusion = f32[16,256,384]{2,0,1:T(8,128)S(1)} fusion(f32[16,256,384]{2,0,1:T(8,128)S(1)} %fusion.123, f32[16,256,384]{2,0,1:T(8,128)} %fusion.98, f32[16,256,384]{2,1,0:T(8,128)S(1)} %bitcast.146, f32[256,384]{1,0:T(8,128)S(1)} %fusion.83, f32[16,16]{1,0:T(8,128)S(1)} %fusion.111), kind=kOutput, calls=%fused_computation.72 | convolution fusion | flops 306708480 | bytes 25560064 | tf_op jit(solution)/shard_map/kab,kl->lab/dot_general | solution.py:48
  499.0 4.6 copy.62
  503.6 4.6 copy.63
  (147 shorter events, 98.8 us)
Async XLA Ops:
  0.6 14.2 %copy-start = (f32[16,256,384]{2,1,0:T(8,128)S(1)}, f32[16,256,384]{2,1,0:T(8,128)}, u32[]{:S(2)}) copy-start(f32[16,256,384]{2,1,0:T(8,128)} %param.7) | copy-start | bytes 18874372
  1.5 9.5 %collective-permute-start = (f32[1,384]{1,0:T(1,128)S(1)}, f32[1,384]{1,0:T(1,128)S(1)}, u32[]{:S(2)}, u32[]{:S(2)}) collective-permute-start(f32[1,384]{1,0:T(1,128)S(1)} %slice.108), channel_id=1, source_target_pairs={{0,8},{8,16},{16,24},{1,9},{9,17},{17,25},{2,10},{10,18},{18,26},{... | collective-permute-start | bytes 4616 | tf_op jit(solution)/shard_map/ppermute | solution.py:18
  7.7 3.3 collective-permute-start.1
  77.1 7.9 %copy-start.3 = (f32[16,256,384]{2,0,1:T(8,128)}, f32[16,256,384]{2,0,1:T(8,128)S(1)}, u32[]{:S(2)}) copy-start(f32[16,256,384]{2,0,1:T(8,128)S(1)} %multiply_multiply_fusion) | copy-start | bytes 18874372
  77.1 4.2 collective-permute-start.3
  79.2 5.7 %collective-permute-start.2 = (f32[16,1,384]{2,0,1:T(8,128)S(1)}, f32[16,1,384]{2,0,1:T(8,128)S(1)}, u32[]{:S(2)}, u32[]{:S(2)}) collective-permute-start(f32[16,1,384]{2,0,1:T(8,128)S(1)} %get-tuple-element.35), channel_id=1, source_target_pairs={{8,0},{16,8},{24,16},{9,1},{17,9},{25,17},{10,2},{18,10},{26,18},{... | collective-permute-start | bytes 73736 | tf_op jit(solution)/shard_map/ppermute | solution.py:31
  87.6 17.3 %copy-start.7 = (f32[256,384]{1,0:T(8,128)S(1)}, f32[256,384]{1,0:T(8,128)}, u32[]{:S(2)}) copy-start(f32[256,384]{1,0:T(8,128)} %param.9) | copy-start | bytes 1179652
  92.9 9.5 %collective-permute-start.5 = (f32[16,258,1]{1,0,2:T(8,128)S(1)}, f32[16,258,1]{1,0,2:T(8,128)S(1)}, u32[]{:S(2)}, u32[]{:S(2)}) collective-permute-start(f32[16,258,1]{1,0,2:T(8,128)S(1)} %copy.32), channel_id=1, source_target_pairs={{0,1},{1,2},{2,3},{3,4},{4,5},{5,6},{6,7},{8,9},{9,10},{10,11},{11... | collective-permute-start | bytes 49544 | tf_op jit(solution)/shard_map/ppermute | solution.py:29
  94.2 5.6 %collective-permute-start.4 = (f32[16,258,1]{1,0,2:T(8,128)S(1)}, f32[16,258,1]{1,0,2:T(8,128)S(1)}, u32[]{:S(2)}, u32[]{:S(2)}) collective-permute-start(f32[16,258,1]{1,0,2:T(8,128)S(1)} %copy.30), channel_id=1, source_target_pairs={{1,0},{2,1},{3,2},{4,3},{5,4},{6,5},{7,6},{9,8},{10,9},{11,10},{12... | collective-permute-start | bytes 49544 | tf_op jit(solution)/shard_map/ppermute | solution.py:31
  102.4 32.2 %slice-start = ((s8[6291456]{0:T(1024)(128)(4,1)}), s8[2097152]{0:T(1024)(128)(4,1)S(1)}, s32[]{:S(2)}) async-start(s8[6291456]{0:T(1024)(128)(4,1)} %bitcast.143), calls=%async_computation | async-start | bytes 4194304
  104.9 29.7 %slice-start.1 = ((s8[6291456]{0:T(1024)(128)(4,1)}), s8[4194304]{0:T(1024)(128)(4,1)S(1)}, s32[]{:S(2)}) async-start(s8[6291456]{0:T(1024)(128)(4,1)} %bitcast.143), calls=%async_computation.1 | async-start | bytes 8388608
  126.5 18.5 %copy-start.2 = (f32[16,256,384]{2,0,1:T(8,128)}, f32[16,256,384]{2,0,1:T(8,128)S(1)}, u32[]{:S(2)}) copy-start(f32[16,256,384]{2,0,1:T(8,128)S(1)} %fusion.14) | copy-start | bytes 18874372
  233.5 3.3 collective-permute-start.7
  234.8 5.7 %collective-permute-start.6 = (f32[16,1,384]{2,0,1:T(8,128)S(1)}, f32[16,1,384]{2,0,1:T(8,128)S(1)}, u32[]{:S(2)}, u32[]{:S(2)}) collective-permute-start(f32[16,1,384]{2,0,1:T(8,128)S(1)} %get-tuple-element.33), channel_id=1, source_target_pairs={{8,0},{16,8},{24,16},{9,1},{17,9},{25,17},{10,2},{18,10},{26,18},{... | collective-permute-start | bytes 73736 | tf_op jit(solution)/shard_map/ppermute | solution.py:31
  248.4 8.2 %collective-permute-start.9 = (f32[16,258,1]{1,0,2:T(8,128)S(1)}, f32[16,258,1]{1,0,2:T(8,128)S(1)}, u32[]{:S(2)}, u32[]{:S(2)}) collective-permute-start(f32[16,258,1]{1,0,2:T(8,128)S(1)} %copy.45), channel_id=1, source_target_pairs={{0,1},{1,2},{2,3},{3,4},{4,5},{5,6},{6,7},{8,9},{9,10},{10,11},{11... | collective-permute-start | bytes 49544 | tf_op jit(solution)/shard_map/ppermute | solution.py:29
  249.7 4.4 collective-permute-start.8
  256.7 30.5 %slice-start.6 = ((s8[6291456]{0:T(1024)(128)(4,1)}), s8[2097152]{0:T(1024)(128)(4,1)S(1)}, s32[]{:S(2)}) async-start(s8[6291456]{0:T(1024)(128)(4,1)} %bitcast.149), calls=%async_computation.6 | async-start | bytes 4194304
  259.2 27.9 %slice-start.7 = ((s8[6291456]{0:T(1024)(128)(4,1)}), s8[4194304]{0:T(1024)(128)(4,1)S(1)}, s32[]{:S(2)}) async-start(s8[6291456]{0:T(1024)(128)(4,1)} %bitcast.149), calls=%async_computation.7 | async-start | bytes 8388608
  279.0 16.5 %copy-start.1 = (f32[16,256,384]{2,0,1:T(8,128)}, f32[16,256,384]{2,0,1:T(8,128)S(1)}, u32[]{:S(2)}) copy-start(f32[16,256,384]{2,0,1:T(8,128)S(1)} %fusion.31) | copy-start | bytes 18874372
  279.0 16.6 %slice-start.4 = ((s8[6291456]{0:T(1024)(128)(4,1)}), s8[4194304]{0:T(1024)(128)(4,1)S(1)}, s32[]{:S(2)}) async-start(s8[6291456]{0:T(1024)(128)(4,1)} %bitcast.147), calls=%async_computation.4 | async-start | bytes 8388608
  287.2 8.4 %slice-start.5 = ((s8[6291456]{0:T(1024)(128)(4,1)}), s8[2097152]{0:T(1024)(128)(4,1)S(1)}, s32[]{:S(2)}) async-start(s8[6291456]{0:T(1024)(128)(4,1)} %bitcast.147), calls=%async_computation.5 | async-start | bytes 4194304
  375.1 3.0 collective-permute-start.11
  376.4 5.7 %collective-permute-start.10 = (f32[16,1,384]{2,0,1:T(8,128)S(1)}, f32[16,1,384]{2,0,1:T(8,128)S(1)}, u32[]{:S(2)}, u32[]{:S(2)}) collective-permute-start(f32[16,1,384]{2,0,1:T(8,128)S(1)} %get-tuple-element.31), channel_id=1, source_target_pairs={{8,0},{16,8},{24,16},{9,1},{17,9},{25,17},{10,2},{18,10},{26,18},{... | collective-permute-start | bytes 73736 | tf_op jit(solution)/shard_map/ppermute | solution.py:31
  390.0 17.0 %copy-start.8 = (f32[256,384]{1,0:T(8,128)S(1)}, f32[256,384]{1,0:T(8,128)}, u32[]{:S(2)}) copy-start(f32[256,384]{1,0:T(8,128)} %param.8) | copy-start | bytes 1179652
  390.0 17.0 %copy-start.9 = (f32[256,384]{1,0:T(8,128)S(1)}, f32[256,384]{1,0:T(8,128)}, u32[]{:S(2)}) copy-start(f32[256,384]{1,0:T(8,128)} %convert_element_type.3) | copy-start | bytes 1179652
  390.1 17.0 %copy-start.10 = (f32[256,384]{1,0:T(8,128)S(1)}, f32[256,384]{1,0:T(8,128)}, u32[]{:S(2)}) copy-start(f32[256,384]{1,0:T(8,128)} %get-tuple-element.20) | copy-start | bytes 1179652
  390.1 17.0 %copy-start.11 = (f32[256,384]{1,0:T(8,128)S(1)}, f32[256,384]{1,0:T(8,128)}, u32[]{:S(2)}) copy-start(f32[256,384]{1,0:T(8,128)} %get-tuple-element.22) | copy-start | bytes 1179652
  390.1 17.0 %copy-start.12 = (f32[256,384]{1,0:T(8,128)S(1)}, f32[256,384]{1,0:T(8,128)}, u32[]{:S(2)}) copy-start(f32[256,384]{1,0:T(8,128)} %get-tuple-element.23) | copy-start | bytes 1179652
  390.1 14.4 %collective-permute-start.13 = (f32[16,258,1]{1,0,2:T(8,128)S(1)}, f32[16,258,1]{1,0,2:T(8,128)S(1)}, u32[]{:S(2)}, u32[]{:S(2)}) collective-permute-start(f32[16,258,1]{1,0,2:T(8,128)S(1)} %copy.56), channel_id=1, source_target_pairs={{0,1},{1,2},{2,3},{3,4},{4,5},{5,6},{6,7},{8,9},{9,10},{10,11},{11... | collective-permute-start | bytes 49544 | tf_op jit(solution)/shard_map/ppermute | solution.py:29
  391.5 10.4 %collective-permute-start.12 = (f32[16,258,1]{1,0,2:T(8,128)S(1)}, f32[16,258,1]{1,0,2:T(8,128)S(1)}, u32[]{:S(2)}, u32[]{:S(2)}) collective-permute-start(f32[16,258,1]{1,0,2:T(8,128)S(1)} %copy.54), channel_id=1, source_target_pairs={{1,0},{2,1},{3,2},{4,3},{5,4},{6,5},{7,6},{9,8},{10,9},{11,10},{12... | collective-permute-start | bytes 49544 | tf_op jit(solution)/shard_map/ppermute | solution.py:31
  429.1 57.8 %slice-start.2 = ((s8[6291456]{0:T(1024)(128)(4,1)}), s8[2097152]{0:T(1024)(128)(4,1)S(1)}, s32[]{:S(2)}) async-start(s8[6291456]{0:T(1024)(128)(4,1)} %bitcast.145), calls=%async_computation.2 | async-start | bytes 4194304
  470.3 16.6 %slice-start.3 = ((s8[6291456]{0:T(1024)(128)(4,1)}), s8[4194304]{0:T(1024)(128)(4,1)S(1)}, s32[]{:S(2)}) async-start(s8[6291456]{0:T(1024)(128)(4,1)} %bitcast.145), calls=%async_computation.3 | async-start | bytes 8388608
  (3 other events, 16.8 us)
